TPU v7x, 128 devices: a whole 4x4x4 slice. The times are simulated.
128 devices in a mesh: vocab: 64 (over x, y, z), width: 2 (over core).
Axes of the slice: x: 4, y: 4, z: 4, core: 2. Of those that a mesh axis runs over, the one named last changes fastest.
Arguments:
- token_grads: bfloat16 [65536, 4608], P('vocab', 'width'), may hold values from -6 to 6
- token_slot: int32 [65536], P('vocab'), may hold values from 0 to 1023, as said below
- slot_rows: int32 [64, 1024], P('vocab'), may hold values from 0 to 1023, as said below
- counts: int32 [64, 64], P('vocab'), may hold values from 1 to 16, as said below
- weights: bfloat16 [65536, 4608], P('vocab', 'width'), may hold values from -0.29882812 to 0.29882812
- moment: bfloat16 [65536, 4608], P('vocab', 'width'), may hold values from -2 to 2
- row_scale: float32 [65536], P('vocab'), may hold values from 0.1 to 4
- row_steps: int32 [65536], P('vocab'), may hold values from 0 to 11
Outputs:
- new_weights: bfloat16 [65536, 4608], P('vocab', 'width')
- new_moment: bfloat16 [65536, 4608], P('vocab', 'width')
- new_scale: float32 [65536], P('vocab')
Inputs may be any that keep to these rules, and one draw needn't show every extreme that they name: `token_slot`: each token names a live slot of its own source. `slot_rows`: within one source and one owner the 16 entries are distinct. `counts`: in every draw some owners receive 16 live slots from every source.
All inputs are finite; a program needn't handle non-finite values.
Results may differ from a plain program's by a relative error of at most 0.0011.
Values may be sent and summed in bfloat16 or wider, within the bound.
A program may use at most 128 MiB of HBM per device.

v0:
```python
import jax
import jax.numpy as jnp
from jax import lax
from jax.sharding import PartitionSpec as P

D = 4608


def over_pieces(value, axis):
    parts = lax.all_gather(value, axis)
    return parts.sum(axis=0)


def shards(token_grads, token_slot, slot_rows, counts, weights, moment, row_scale, row_steps):
    owners = lax.axis_size("vocab")
    slots_all = slot_rows.shape[1]
    cap = slots_all // owners
    half = token_grads.shape[1]
    rows_own = weights.shape[0]
    placing = token_slot[None, :] == jnp.arange(slots_all, dtype=jnp.int32)[:, None]
    slot_grads = jnp.dot(
        placing.astype(jnp.bfloat16), token_grads, preferred_element_type=jnp.float32
    ).astype(jnp.bfloat16)
    within = jnp.arange(cap, dtype=jnp.int32)
    live = within[None, :] < counts[0][:, None]
    named = jnp.where(live, slot_rows[0].reshape(owners, cap), -1)
    outgoing = slot_grads.reshape(owners, cap, half)
    received, received_rows = (
        lax.all_to_all(outgoing, "vocab", split_axis=0, concat_axis=0, tiled=True),
        lax.all_to_all(named, "vocab", split_axis=0, concat_axis=0, tiled=True),
    )
    flat = received.reshape(owners * cap, half)
    flat_rows = received_rows.reshape(owners * cap)
    table = flat_rows[None, :] == jnp.arange(rows_own, dtype=jnp.int32)[:, None]
    grad = jnp.dot(table.astype(jnp.bfloat16), flat, preferred_element_type=jnp.float32)
    hits = jnp.sum(table.astype(jnp.int32), axis=1)
    touched = hits > 0
    partial_sum = jnp.sum(grad * grad, axis=1)
    square = over_pieces(partial_sum, "width") / D
    step_count = (row_steps + 1).astype(jnp.float32)
    old_moment = moment.astype(jnp.float32)
    first = jnp.where(touched[:, None], 0.9 * old_moment + 0.1 * grad, old_moment)
    second = jnp.where(touched, 0.95 * row_scale + 0.05 * square, row_scale)
    fix_first = 1.0 - jnp.power(jnp.float32(0.9), step_count)
    fix_second = 1.0 - jnp.power(jnp.float32(0.95), step_count)
    denom = jnp.sqrt(second / fix_second) + 1e-08
    old = weights.astype(jnp.float32)
    stepped = old - 0.01 * (first / fix_first[:, None] / denom[:, None] + 0.1 * old)
    new_weights = jnp.where(touched[:, None], stepped, old).astype(jnp.bfloat16)
    return (new_weights, first.astype(jnp.bfloat16), second)


def solution(mesh):
    return jax.shard_map(
        shards,
        mesh=mesh,
        in_specs=(
            P("vocab", "width"),
            P("vocab"),
            P("vocab", None),
            P("vocab", None),
            P("vocab", "width"),
            P("vocab", "width"),
            P("vocab"),
            P("vocab"),
        ),
        out_specs=(P("vocab", "width"), P("vocab", "width"), P("vocab")),
        check_vma=False,
    )
```

profile of v0, /device:TPU:83, one launch (start us, length us, event | category | flops | bytes accessed | tf_op | source)
XLA Modules:
  0.0 123.9 jit_solution(2142956770170462065)
XLA Ops:
  0.6 0.5 broadcast.57
  1.1 1.3 %reduce.6 = s32[1024]{0:T(1024)S(1)} reduce(s32[1,1024]{1,0:T(1,128)} %param.10, s32[]{:T(128)} %broadcast.57), dimensions={0}, to_apply=%param.10.reduce_sub_computation.3 | reduce | bytes 8196 | tf_op args[2]
  2.5 0.1 reshape_squeeze.3
  2.6 1.3 %fusion.8 = s32[64,1,16]{2,0,1:T(8,128)} fusion(s32[64,1,16]{2,0,1:T(8,128)S(1)} %reshape_squeeze.3, s32[64]{0:T(128)} %bitcast.7), kind=kLoop, calls=%fused_computation.18 | loop fusion | flops 2048 | bytes 8448 | tf_op jit(solution)/shard_map/jit(_where)/select_n | solution.py:26
  3.9 9.9 %all-to-all-start = ((s32[64,1,16]{2,1,0:T(1,128)}), s32[64,1,16]{2,1,0:T(1,128)S(1)}, u32[]{:S(2)}, u32[]{:S(2)}) async-start(s32[64,1,16]{2,1,0:T(1,128)} %bitcast.1), calls=%async_computation | async-start | bytes 65536 | tf_op jit(solution)/shard_map/all_to_all | solution.py:30
  13.8 9.1 %convolution_convert_fusion = bf16[1024,2304]{1,0:T(8,128)(2,1)} fusion(bf16[1024,2304]{1,0:T(8,128)(2,1)} %param.8, s32[1024]{0:T(1024)} %param.9), kind=kOutput, calls=%fused_computation.9 | convolution fusion | flops 4835246080 | bytes 9441280 | tf_op jit(solution)/shard_map/dot_general | solution.py:21
  22.9 0.0 all-to-all-done
  22.9 9.9 %all-to-all-start.1 = ((bf16[64,16,2304]{2,1,0:T(8,128)(2,1)}), bf16[64,16,2304]{2,1,0:T(8,128)(2,1)}, u32[]{:S(2)}, u32[]{:S(2)}) async-start(bf16[64,16,2304]{2,1,0:T(8,128)(2,1)} %bitcast.6), calls=%async_computation.1 | async-start | bytes 9437184 | tf_op jit(solution)/shard_map/all_to_all | solution.py:29
  32.9 0.7 reduce.7
  33.6 0.1 eq.28
  33.7 0.5 convert_reduce_fusion
  34.2 61.7 %all-to-all-done.1 = bf16[64,16,2304]{2,1,0:T(8,128)(2,1)} async-done(((bf16[64,16,2304]{2,1,0:T(8,128)(2,1)}), bf16[64,16,2304]{2,1,0:T(8,128)(2,1)}, u32[]{:S(2)}, u32[]{:S(2)}) %all-to-all-start.1) | async-done | bytes 4718624 | tf_op jit(solution)/shard_map/all_to_all | solution.py:29
  95.8 0.0 copy-start
  95.8 0.0 copy-start.1
  95.8 9.9 %multiply_reduce_fusion = (f32[1024]{0:T(1024)S(1)}, f32[1024,2304]{1,0:T(8,128)}) fusion(bf16[1024,2304]{1,0:T(8,128)(2,1)} %bitcast.3, s32[1024]{0:T(1024)S(1)} %eq.28), kind=kOutput, calls=%fused_computation.8 | convolution fusion | flops 4837604352 | bytes 14163968 | tf_op jit(solution)/shard_map/dot_general | solution.py:35
  105.8 4.1 %all-gather = f32[2048]{0:T(1024)S(1)} all-gather(f32[1024]{0:T(1024)S(1)} %get-tuple-element.8), channel_id=2, replica_groups=mesh['vocab'=64,'width'=2] {'width'}, dimensions={0}, use_global_device_ids=true | all-gather | bytes 12288 | tf_op jit(solution)/shard_map/all_gather | solution.py:10
  109.9 0.0 copy-done
  109.9 0.0 copy-done.1
  109.9 0.6 add_multiply_fusion
  110.5 13.3 %fusion.4 = (bf16[1024,2304]{1,0:T(8,128)(2,1)}, bf16[1024,2304]{1,0:T(8,128)(2,1)}) fusion(f32[1024,2304]{1,0:T(8,128)} %get-tuple-element.9, bf16[1024,2304]{1,0:T(8,128)(2,1)} %param.13, pred[1024]{0:T(1024)(128)(4,1)S(1)} %get-tuple-element.5, f32[1024]{0:T(1024)S(1)} %get-tuple-element.3, bf16[1024,2304]{1,0:T(8,128)(2,1)} %param.12), kind=kLoop, calls=%fused_computation.10 | loop fusion | flops 33030144 | bytes 28316672 | tf_op jit(solution)/shard_map/convert_element_type | solution.py:50
  (2 shorter events, 0.0 us)
Async XLA Ops:
  3.9 19.0 %all-to-all-start = ((s32[64,1,16]{2,1,0:T(1,128)}), s32[64,1,16]{2,1,0:T(1,128)S(1)}, u32[]{:S(2)}, u32[]{:S(2)}) async-start(s32[64,1,16]{2,1,0:T(1,128)} %bitcast.1), calls=%async_computation | async-start | bytes 65536 | tf_op jit(solution)/shard_map/all_to_all | solution.py:30
  22.9 72.9 %all-to-all-start.1 = ((bf16[64,16,2304]{2,1,0:T(8,128)(2,1)}), bf16[64,16,2304]{2,1,0:T(8,128)(2,1)}, u32[]{:S(2)}, u32[]{:S(2)}) async-start(bf16[64,16,2304]{2,1,0:T(8,128)(2,1)} %bitcast.6), calls=%async_computation.1 | async-start | bytes 9437184 | tf_op jit(solution)/shard_map/all_to_all | solution.py:29
  95.8 14.1 %copy-start = (s32[1024]{0:T(1024)S(1)}, s32[1024]{0:T(1024)}, u32[]{:S(2)}) copy-start(s32[1024]{0:T(1024)} %param.15) | copy-start | bytes 12292
  95.8 14.1 %copy-start.1 = (f32[1024]{0:T(1024)S(1)}, f32[1024]{0:T(1024)}, u32[]{:S(2)}) copy-start(f32[1024]{0:T(1024)} %param.14) | copy-start | bytes 12292
where the time goes:
time: 124 us
  waiting for transfers between devices  61.7 us (50%)
  starting transfers between devices  19.8 us (16%)
  matrix products  19.1 us (15%)
  other arithmetic  17.9 us (14%)
  blocking collectives  4.12 us (3%)
    all_to_all x1, waiting for transfers between devices, shards(): lax.all_to_all(outgoing, 'vocab', split_axis=0, concat_axis=0, tiled=True)  61.7 us
    convert_element_type x1, other arithmetic, shards(): return (new_weights, first.astype(jnp.bfloat16), second)  13.3 us
    all_to_all x1, starting transfers between devices, shards(): lax.all_to_all(outgoing, 'vocab', split_axis=0, concat_axis=0, tiled=True)  9.94 us
    dot_general x1, matrix products, shards(): jnp.dot(table.astype(jnp.bfloat16), flat, preferred_element_type=jnp.floa...  9.94 us
    all_to_all x1, starting transfers between devices, shards(): lax.all_to_all(named, 'vocab', split_axis=0, concat_axis=0, tiled=True)  9.86 us
    dot_general x1, matrix products, shards(): jnp.dot(placing.astype(jnp.bfloat16), token_grads, preferred_element_type...  9.13 us
    all_gather x1, blocking collectives, over_pieces(): parts = lax.all_gather(value, axis)  4.12 us
  transfers between devices with their start and end apart: 2, of which 1 were waited for; matrix products, arithmetic and copies ran while one was open for 8% of the time, Pallas kernels for 0%

commit v1 on v0

v1 whole, which is shorter than its diff:
```python
import functools
import jax
import jax.numpy as jnp
from jax import lax
from jax.experimental import pallas as pl
from jax.experimental.pallas import tpu as pltpu
from jax.sharding import PartitionSpec as P

D = 4608
HALF = 2304
ROWS = 1024
CAP = 16
GROUPS = 3
PER = 3
CW = HALF // (GROUPS * PER)
CHUNKS = GROUPS * PER
MESH = pl.DeviceIdType.MESH
ORDERS = ((0, 1, 2), (1, 2, 0), (2, 0, 1))


def to_column(row):
    eye = lax.broadcasted_iota(jnp.int32, (128, 128), 0) == lax.broadcasted_iota(jnp.int32, (128, 128), 1)
    parts = [
        jnp.sum(jnp.where(eye, row[g : g + 1, :], 0.0), axis=1, keepdims=True) for g in range(8)
    ]
    return jnp.concatenate(parts, axis=0)


def to_row(column):
    eye = lax.broadcasted_iota(jnp.int32, (128, 128), 0) == lax.broadcasted_iota(jnp.int32, (128, 128), 1)
    parts = [
        jnp.sum(jnp.where(eye, column[g * 128 : g * 128 + 128, :], 0.0), axis=0, keepdims=True)
        for g in range(8)
    ]
    return jnp.concatenate(parts, axis=0)


def exchange(
    tg, ts, srows, cnts, rscale, rsteps,
    grad, coef, scale,
    tgv, send, r1, r2, r3, onehot, ms, m1, m2, m3, acc, sq_out, sq_in,
    load_sem, send_sem, recv_sem, msend_sem, mrecv_sem, sq_sem,
):
    me = lax.axis_index("vocab")
    core = lax.axis_index("width")
    at = (me // 16, (me // 4) % 4, me % 4)
    stride = (16, 4, 1)

    def peer(dim, delta):
        there = (at[dim] + delta) % 4
        return there, (me + (there - at[dim]) * stride[dim], core)

    def load(c):
        return pltpu.make_async_copy(tg.at[:, pl.ds(c * CW, CW)], tgv.at[c], load_sem.at[c])

    issue = [g * PER + k for k in range(PER) for g in range(GROUPS)]
    for c in issue:
        load(c).start()

    barrier = pltpu.get_barrier_semaphore()
    for dim in range(3):
        for delta in (1, 2, 3):
            pl.semaphore_signal(barrier, inc=1, device_id=peer(dim, delta)[1], device_id_type=MESH)
    partner = (me, 1 - core)
    pl.semaphore_signal(barrier, inc=1, device_id=partner, device_id_type=MESH)

    for rb in range(8):
        rows = lax.broadcasted_iota(jnp.int32, (128, 128), 0) + rb * 128
        for g in range(8):
            onehot[0, pl.ds(rb * 128, 128), pl.ds(g * 128, 128)] = (
                (rows == ts[g : g + 1, :]).astype(jnp.float32).astype(jnp.bfloat16)
            )

    def leaving(buf, phase, order, c, there):
        dim = order[phase]
        if phase == 0:
            return (buf.at[c, there], buf.at[c, :, there], buf.at[c, :, :, there])[dim]
        if phase == 1:
            rest = sorted(order[1:])
            return buf.at[c, :, there] if rest[0] == dim else buf.at[c, :, :, there]
        return buf.at[c, :, :, there]

    def landing(buf, phase, order, c):
        dim = order[phase]
        if phase == 0:
            return buf.at[c, at[dim]]
        if phase == 1:
            seen = sorted(order[:2])
            return buf.at[c, at[dim]] if seen[0] == dim else buf.at[c, :, at[dim]]
        return (buf.at[c, at[dim]], buf.at[c, :, at[dim]], buf.at[c, :, :, at[dim]])[dim]

    bufs = (send, r1, r2, r3)
    mbufs = (ms, m1, m2, m3)

    def forward(phase, c, order, kind, ssem, rsem):
        src, dst = kind[phase], kind[phase + 1]
        dim = order[phase]
        for delta in (2, 1, 3):
            there, device = peer(dim, delta)
            pltpu.make_async_remote_copy(
                src_ref=leaving(src, phase, order, c, there),
                dst_ref=landing(dst, phase, order, c),
                send_sem=ssem, recv_sem=rsem, device_id=device, device_id_type=MESH,
            ).start()
        landing(dst, phase, order, c)[...] = leaving(src, phase, order, c, at[dim])[...]

    def take(kind, sem):
        whole = kind[0].at[0, pl.ds(0, 3)]
        pltpu.make_async_copy(whole, whole, sem).wait()

    lane_g = lax.broadcasted_iota(jnp.int32, (64, 128), 1) // CAP
    own_g = lax.broadcasted_iota(jnp.int32, (64, 128), 0) % 8
    spread = (lane_g == own_g).astype(jnp.float32)
    owner8 = lax.broadcasted_iota(jnp.int32, (8, 64), 1) // 8
    by_block = jnp.where(
        owner8 == lax.broadcasted_iota(jnp.int32, (8, 64), 0), cnts[...].astype(jnp.float32), 0.0
    )
    count = jnp.dot(by_block, spread, preferred_element_type=jnp.float32)
    lanes = lax.broadcasted_iota(jnp.int32, (8, 128), 1)
    names = jnp.concatenate([srows[:, g * 128 : g * 128 + 128] for g in range(8)], axis=0)
    names = jnp.where((lanes % CAP).astype(jnp.float32) < count, names + 1, 0)
    for j in range(8):
        turned = pltpu.roll(names, ((me % 8) - j + 8) % 8 * CAP, 1)
        turned = jnp.where(lanes // CAP == me % 8, turned, 0)
        for g in range(8):
            o = 8 * g + j
            ms[0, o // 16, (o // 4) % 4, o % 4] = turned[g : g + 1, :]

    pl.semaphore_wait(barrier, 10)
    forward(0, 0, ORDERS[0], mbufs, msend_sem.at[0], mrecv_sem.at[0])

    for c in issue:
        load(c).wait()
        send[c] = (
            jnp.dot(onehot[0], tgv[c], preferred_element_type=jnp.float32)
            .astype(jnp.bfloat16)
            .reshape(4, 4, 4, CAP, CW)
        )
        forward(0, c, ORDERS[c // PER], bufs, send_sem.at[0, c], recv_sem.at[0, c])

    take(mbufs, mrecv_sem.at[0])
    forward(1, 0, ORDERS[0], mbufs, msend_sem.at[1], mrecv_sem.at[1])
    for n, c in enumerate(issue):
        take(bufs, recv_sem.at[0, c])
        forward(1, c, ORDERS[c // PER], bufs, send_sem.at[1, c], recv_sem.at[1, c])
        if n == 2:
            take(mbufs, mrecv_sem.at[1])
            forward(2, 0, ORDERS[0], mbufs, msend_sem.at[2], mrecv_sem.at[2])
    for c in issue:
        take(bufs, recv_sem.at[1, c])
        forward(2, c, ORDERS[c // PER], bufs, send_sem.at[2, c], recv_sem.at[2, c])

    take(mbufs, mrecv_sem.at[2])
    named = m3[0].reshape(8, 8, 128).sum(axis=1)
    touched_parts = []
    for rb in range(8):
        rows = lax.broadcasted_iota(jnp.int32, (128, 128), 0) + (rb * 128 + 1)
        any_hit = jnp.zeros((128, 128), jnp.float32)
        for g in range(8):
            hit = (rows == named[g : g + 1, :]).astype(jnp.float32)
            onehot[1, pl.ds(rb * 128, 128), pl.ds(g * 128, 128)] = hit.astype(jnp.bfloat16)
            any_hit = jnp.maximum(any_hit, hit)
        touched_parts.append(jnp.max(any_hit, axis=1, keepdims=True))
    touched = to_row(jnp.concatenate(touched_parts, axis=0))
    steps = (rsteps[...] + 1).astype(jnp.float32)
    fix_first = 1.0 - jnp.exp(steps * jnp.log(jnp.float32(0.9)))
    fix_second = 1.0 - jnp.exp(steps * jnp.log(jnp.float32(0.95)))

    for n, c in enumerate(issue):
        take(bufs, recv_sem.at[2, c])
        for rb in range(8):
            part = jnp.dot(
                onehot[1, pl.ds(rb * 128, 128), :], r3[c].reshape(ROWS, CW), preferred_element_type=jnp.float32
            )
            grad[pl.ds(rb * 128, 128), pl.ds(c * CW, CW)] = part
            squares = part * part
            folded = squares[:, :128]
            for q in range(1, CW // 128):
                folded = folded + squares[:, q * 128 : q * 128 + 128]
            if n == 0:
                acc[pl.ds(rb * 128, 128), :] = folded
            else:
                acc[pl.ds(rb * 128, 128), :] += folded

    mine = to_row(jnp.sum(acc[...], axis=1, keepdims=True))
    sq_out[...] = mine
    swap = pltpu.make_async_remote_copy(
        src_ref=sq_out, dst_ref=sq_in, send_sem=sq_sem.at[0], recv_sem=sq_sem.at[1],
        device_id=partner, device_id_type=MESH,
    )
    swap.start()

    whole = send.at[0, pl.ds(0, 3)]
    for phase in range(3):
        for c in range(CHUNKS):
            pltpu.make_async_copy(whole, whole, send_sem.at[phase, c]).wait()
        pltpu.make_async_copy(ms.at[0, pl.ds(0, 3)], ms.at[0, pl.ds(0, 3)], msend_sem.at[phase]).wait()
    swap.wait()

    square = (mine + sq_in[...]) / D
    live = touched > 0.0
    second = jnp.where(live, 0.95 * rscale[...] + 0.05 * square, rscale[...])
    scale[...] = second
    denom = jnp.sqrt(second / fix_second) + 1e-08
    rate = jnp.where(live, 0.01 / (fix_first * denom), 0.0)
    keep = jnp.where(live, 0.9, 1.0)
    decay = jnp.where(live, 1.0 - 0.01 * 0.1, 1.0)
    lane = lax.broadcasted_iota(jnp.int32, (ROWS, 128), 1)
    coef[...] = jnp.where(
        lane == 0, to_column(keep), jnp.where(lane == 1, to_column(decay), to_column(rate))
    )


def update(grad, coef, weights, moment, new_weights, new_moment):
    keep = coef[:, 0:1]
    decay = coef[:, 1:2]
    rate = coef[:, 2:3]
    first = keep * moment[...].astype(jnp.float32) + 0.1 * grad[...]
    new_moment[...] = first.astype(jnp.bfloat16)
    new_weights[...] = (decay * weights[...].astype(jnp.float32) - rate * first).astype(jnp.bfloat16)


def shards(token_grads, token_slot, slot_rows, counts, weights, moment, row_scale, row_steps):
    vmem = pl.BlockSpec(memory_space=pltpu.VMEM)
    block = (4, 4, 4, CAP, CW)
    bf16, f32, i32 = jnp.bfloat16, jnp.float32, jnp.int32
    grad, coef, scale = pl.pallas_call(
        exchange,
        name="exchange",
        out_shape=(
            jax.ShapeDtypeStruct((ROWS, HALF), f32),
            jax.ShapeDtypeStruct((ROWS, 128), f32),
            jax.ShapeDtypeStruct((8, 128), f32),
        ),
        in_specs=[pl.BlockSpec(memory_space=pl.ANY)] + [vmem] * 5,
        out_specs=(vmem, vmem, vmem),
        scratch_shapes=[
            pltpu.VMEM((CHUNKS, ROWS, CW), bf16),
            pltpu.VMEM((CHUNKS,) + block, bf16),
            pltpu.VMEM((CHUNKS,) + block, bf16),
            pltpu.VMEM((CHUNKS,) + block, bf16),
            pltpu.VMEM((CHUNKS,) + block, bf16),
            pltpu.VMEM((2, ROWS, ROWS), bf16),
            pltpu.VMEM((1, 4, 4, 4, 1, 128), i32),
            pltpu.VMEM((1, 4, 4, 4, 1, 128), i32),
            pltpu.VMEM((1, 4, 4, 4, 1, 128), i32),
            pltpu.VMEM((1, 4, 4, 4, 1, 128), i32),
            pltpu.VMEM((ROWS, 128), f32),
            pltpu.VMEM((8, 128), f32),
            pltpu.VMEM((8, 128), f32),
            pltpu.SemaphoreType.DMA((CHUNKS,)),
            pltpu.SemaphoreType.DMA((3, CHUNKS)),
            pltpu.SemaphoreType.DMA((3, CHUNKS)),
            pltpu.SemaphoreType.DMA((3,)),
            pltpu.SemaphoreType.DMA((3,)),
            pltpu.SemaphoreType.DMA((2,)),
        ],
        compiler_params=pltpu.CompilerParams(
            collective_id=0, has_side_effects=True, vmem_limit_bytes=48 * 1024 * 1024
        ),
        cost_estimate=pl.CostEstimate(flops=10**10, bytes_accessed=2 * 10**7, transcendentals=0),
    )(
        token_grads, token_slot.reshape(8, 128), slot_rows, counts,
        row_scale.reshape(8, 128), row_steps.reshape(8, 128),
    )
    tall = 128
    wide = pl.BlockSpec((tall, HALF), lambda i: (i, 0))
    new_weights, new_moment = pl.pallas_call(
        update,
        name="update",
        grid=(ROWS // tall,),
        out_shape=(jax.ShapeDtypeStruct((ROWS, HALF), bf16), jax.ShapeDtypeStruct((ROWS, HALF), bf16)),
        in_specs=[wide, pl.BlockSpec((tall, 128), lambda i: (i, 0)), wide, wide],
        out_specs=(wide, wide),
        cost_estimate=pl.CostEstimate(flops=2 * 10**7, bytes_accessed=3 * 10**7, transcendentals=0),
    )(grad, coef, weights, moment)
    return (new_weights, new_moment, scale.reshape(ROWS))


def solution(mesh):
    return jax.shard_map(
        shards,
        mesh=mesh,
        in_specs=(
            P("vocab", "width"),
            P("vocab"),
            P("vocab", None),
            P("vocab", None),
            P("vocab", "width"),
            P("vocab", "width"),
            P("vocab"),
            P("vocab"),
        ),
        out_specs=(P("vocab", "width"), P("vocab", "width"), P("vocab")),
        check_vma=False,
    )
```

time: 124 us -> 92.4 us (0.75)
  the two profiles are of different devices: /device:TPU:83 before, /device:TPU:1 now
where the time goes in v1:
time: 92.4 us; the launch traced here: 92 us
  Pallas kernels  84.3 us (91%)
  local copies, waits for them, and re-layouts  7.11 us (8%)
    pallas_call x1, Pallas kernels, shards(): pl.pallas_call(exchange, name='exchange', out_shape=(jax.ShapeDtypeStruct...  71.4 us
    pallas_call x1, Pallas kernels, shards(): pl.pallas_call(update, name='update', grid=(ROWS // tall,), out_shape=(ja...  12.9 us
    unnamed x15, local copies, waits for them, and re-layouts  7.11 us

profile of v1, /device:TPU:1, one launch (start us, length us, event | category | flops | bytes accessed | tf_op | source)
XLA Modules:
  0.0 92.0 jit_solution(6388434797600876953)
XLA Ops:
  0.6 0.0 copy-start.1
  0.6 2.3 %copy-done.1 = bf16[1024,2304]{1,0:T(8,128)(2,1)S(1)} copy-done((bf16[1024,2304]{1,0:T(8,128)(2,1)S(1)}, bf16[1024,2304]{1,0:T(8,128)(2,1)}, u32[]{:S(2)}) %copy-start.1) | copy-done | bytes 4718616
  3.0 0.0 copy-start.2
  3.0 0.7 copy-done.2
  3.7 0.0 copy-start.3
  3.7 0.7 copy-done.3
  4.3 0.0 copy-start.4
  4.3 0.7 copy-done.4
  5.0 0.0 copy-start.5
  5.0 0.7 copy-done.5
  5.7 0.0 copy-start.6
  5.7 0.7 copy-done.6
  6.4 71.4 %exchange.1 = (f32[1024,2304]{1,0:T(8,128)}, f32[1024,128]{1,0:T(8,128)S(1)}, f32[8,128]{1,0:T(8,128)S(1)}) custom-call(bf16[1024,2304]{1,0:T(8,128)(2,1)S(1)} %copy-done.1, s32[8,128]{1,0:T(8,128)S(1)} %bitcast.5, s32[1,1024]{1,0:T(1,128)S(1)} %copy-done.3, s32[1,64]{1,0:T(1,128)S(1)} %copy-done.6, f32[8,128]{1,0:T(8,128)S(1)} %bitcast.6, s32[8,128]{1,0:T(8,128)S(1)} %bitcast.7), custom_call_target="tpu_custom_call" | custom-call | flops 10000000000 | bytes 20000000 | tf_op jit(solution)/shard_map/exchange/pallas_call | solution.py:227
  77.8 0.0 copy-start
  77.8 0.8 copy-done
  78.6 12.9 %update.1 = (bf16[1024,2304]{1,0:T(8,128)(2,1)}, bf16[1024,2304]{1,0:T(8,128)(2,1)}) custom-call(f32[1024,2304]{1,0:T(8,128)} %get-tuple-element.8.grad, f32[1024,128]{1,0:T(8,128)} %copy-done, bf16[1024,2304]{1,0:T(8,128)(2,1)} %weights.1, bf16[1024,2304]{1,0:T(8,128)(2,1)} %moment.1), custom_call_target="tpu_custom_call" | custom-call | flops 20000000 | bytes 30000000 | tf_op jit(solution)/shard_map/update/pallas_call | solution.py:268
  91.4 0.6 copy.12
Async XLA Ops:
  0.6 2.3 %copy-start.1 = (bf16[1024,2304]{1,0:T(8,128)(2,1)S(1)}, bf16[1024,2304]{1,0:T(8,128)(2,1)}, u32[]{:S(2)}) copy-start(bf16[1024,2304]{1,0:T(8,128)(2,1)} %tg.1) | copy-start | bytes 14155780
  3.0 0.7 copy-start.2
  3.7 0.7 copy-start.3
  4.3 0.7 copy-start.4
  5.0 0.7 copy-start.5
  5.7 0.7 copy-start.6
  77.8 0.8 copy-start

commit v2 on v1

v2 whole, which is shorter than its diff:
```python
import functools
import jax
import jax.numpy as jnp
from jax import lax
from jax.experimental import pallas as pl
from jax.experimental.pallas import tpu as pltpu
from jax.sharding import PartitionSpec as P

D = 4608
HALF = 2304
ROWS = 1024
CAP = 16
GROUPS = 3
WIDTHS = (128, 256, 256, 128)
PER = len(WIDTHS)
CHUNKS = GROUPS * PER
WIDTH = WIDTHS * GROUPS
FIRST = tuple(sum(WIDTH[:c]) for c in range(CHUNKS))
TALL = 128
MESH = pl.DeviceIdType.MESH
ORDERS = ((0, 1, 2), (1, 2, 0), (2, 0, 1))


def to_row(column):
    eye = lax.broadcasted_iota(jnp.int32, (128, 128), 0) == lax.broadcasted_iota(jnp.int32, (128, 128), 1)
    parts = [
        jnp.sum(jnp.where(eye, column[g * 128 : g * 128 + 128, :], 0.0), axis=0, keepdims=True)
        for g in range(8)
    ]
    return jnp.concatenate(parts, axis=0)


def exchange(
    tg, ts_hbm, srows_hbm, cnts_hbm, rscale_hbm, rsteps_hbm, weights, moment,
    first, coef, scale, weights_v,
    ts, srows, cnts, rscale, rsteps, moment_v, keep,
    tgv, send, r1, r2, r3, onehot, ms, m1, m2, m3, acc, sq_out, sq_in,
    small_sem, wide_sem, load_sem, send_sem, recv_sem, msend_sem, mrecv_sem, sq_sem,
):
    me = lax.axis_index("vocab")
    core = lax.axis_index("width")
    at = (me // 16, (me // 4) % 4, me % 4)
    stride = (16, 4, 1)

    def peer(dim, delta):
        there = (at[dim] + delta) % 4
        return there, (me + (there - at[dim]) * stride[dim], core)

    def load(c):
        return pltpu.make_async_copy(tg.at[:, pl.ds(FIRST[c], WIDTH[c])], tgv[c], load_sem.at[c])

    issue = [g * PER + k for k in range(PER) for g in range(GROUPS)]
    small = [
        pltpu.make_async_copy(src, dst, small_sem.at[i])
        for i, (src, dst) in enumerate(
            ((ts_hbm, ts), (srows_hbm, srows), (cnts_hbm, cnts), (rscale_hbm, rscale), (rsteps_hbm, rsteps))
        )
    ]
    for copy in small:
        copy.start()
    for c in issue:
        load(c).start()
    wide = [
        pltpu.make_async_copy(src, dst, wide_sem.at[i])
        for i, (src, dst) in enumerate(((weights, weights_v), (moment, moment_v)))
    ]

    barrier = pltpu.get_barrier_semaphore()
    for dim in range(3):
        for delta in (1, 2, 3):
            pl.semaphore_signal(barrier, inc=1, device_id=peer(dim, delta)[1], device_id_type=MESH)
    partner = (me, 1 - core)
    pl.semaphore_signal(barrier, inc=1, device_id=partner, device_id_type=MESH)

    for copy in small:
        copy.wait()
    for rb in range(8):
        rows = lax.broadcasted_iota(jnp.int32, (128, 128), 0) + rb * 128
        for g in range(8):
            onehot[0, pl.ds(rb * 128, 128), pl.ds(g * 128, 128)] = (
                (rows == ts[g : g + 1, :]).astype(jnp.float32).astype(jnp.bfloat16)
            )

    def leaving(buf, phase, order, c, there):
        dim = order[phase]
        if phase == 0:
            return (buf[c].at[there], buf[c].at[:, there], buf[c].at[:, :, there])[dim]
        if phase == 1:
            rest = sorted(order[1:])
            return buf[c].at[:, there] if rest[0] == dim else buf[c].at[:, :, there]
        return buf[c].at[:, :, there]

    def landing(buf, phase, order, c):
        dim = order[phase]
        if phase == 0:
            return buf[c].at[at[dim]]
        if phase == 1:
            seen = sorted(order[:2])
            return buf[c].at[at[dim]] if seen[0] == dim else buf[c].at[:, at[dim]]
        return (buf[c].at[at[dim]], buf[c].at[:, at[dim]], buf[c].at[:, :, at[dim]])[dim]

    bufs = (send, r1, r2, r3)
    mbufs = ((ms,), (m1,), (m2,), (m3,))

    def forward(phase, c, order, kind, ssem, rsem):
        src, dst = kind[phase], kind[phase + 1]
        dim = order[phase]
        for delta in (2, 1, 3):
            there, device = peer(dim, delta)
            pltpu.make_async_remote_copy(
                src_ref=leaving(src, phase, order, c, there),
                dst_ref=landing(dst, phase, order, c),
                send_sem=ssem, recv_sem=rsem, device_id=device, device_id_type=MESH,
            ).start()
        landing(dst, phase, order, c)[...] = leaving(src, phase, order, c, at[dim])[...]

    def take(kind, c, sem):
        whole = kind[0][c].at[pl.ds(0, 3)]
        pltpu.make_async_copy(whole, whole, sem).wait()

    lane_g = lax.broadcasted_iota(jnp.int32, (64, 128), 1) // CAP
    own_g = lax.broadcasted_iota(jnp.int32, (64, 128), 0) % 8
    spread = (lane_g == own_g).astype(jnp.float32)
    owner8 = lax.broadcasted_iota(jnp.int32, (8, 64), 1) // 8
    by_block = jnp.where(
        owner8 == lax.broadcasted_iota(jnp.int32, (8, 64), 0), cnts[...].astype(jnp.float32), 0.0
    )
    count = jnp.dot(by_block, spread, preferred_element_type=jnp.float32)
    lanes = lax.broadcasted_iota(jnp.int32, (8, 128), 1)
    names = jnp.concatenate([srows[:, g * 128 : g * 128 + 128] for g in range(8)], axis=0)
    names = jnp.where((lanes % CAP).astype(jnp.float32) < count, names + 1, 0)
    for j in range(8):
        turned = pltpu.roll(names, ((me % 8) - j + 8) % 8 * CAP, 1)
        turned = jnp.where(lanes // CAP == me % 8, turned, 0)
        for g in range(8):
            o = 8 * g + j
            ms[o // 16, (o // 4) % 4, o % 4] = turned[g : g + 1, :]

    pl.semaphore_wait(barrier, 10)
    forward(0, 0, ORDERS[0], mbufs, msend_sem.at[0], mrecv_sem.at[0])

    for c in issue:
        load(c).wait()
        send[c][...] = (
            jnp.dot(onehot[0], tgv[c][...], preferred_element_type=jnp.float32)
            .astype(jnp.bfloat16)
            .reshape(4, 4, 4, CAP, WIDTH[c])
        )
        forward(0, c, ORDERS[c // PER], bufs, send_sem.at[0, c], recv_sem.at[0, c])

    for copy in wide:
        copy.start()
    take(mbufs, 0, mrecv_sem.at[0])
    forward(1, 0, ORDERS[0], mbufs, msend_sem.at[1], mrecv_sem.at[1])
    for n, c in enumerate(issue):
        take(bufs, c, recv_sem.at[0, c])
        forward(1, c, ORDERS[c // PER], bufs, send_sem.at[1, c], recv_sem.at[1, c])
        if n == 2:
            take(mbufs, 0, mrecv_sem.at[1])
            forward(2, 0, ORDERS[0], mbufs, msend_sem.at[2], mrecv_sem.at[2])
    for c in issue:
        take(bufs, c, recv_sem.at[1, c])
        forward(2, c, ORDERS[c // PER], bufs, send_sem.at[2, c], recv_sem.at[2, c])

    take(mbufs, 0, mrecv_sem.at[2])
    named = m3[...].reshape(8, 8, 128).sum(axis=1)
    touched_parts = []
    for rb in range(8):
        rows = lax.broadcasted_iota(jnp.int32, (128, 128), 0) + (rb * 128 + 1)
        any_hit = jnp.zeros((128, 128), jnp.float32)
        for g in range(8):
            hit = (rows == named[g : g + 1, :]).astype(jnp.float32)
            onehot[1, pl.ds(rb * 128, 128), pl.ds(g * 128, 128)] = hit.astype(jnp.bfloat16)
            any_hit = jnp.maximum(any_hit, hit)
        hit_column = jnp.max(any_hit, axis=1, keepdims=True)
        touched_parts.append(hit_column)
        keep[pl.ds(rb * 128, 128), :] = jnp.broadcast_to(1.0 - 0.1 * hit_column, (128, 128))
    touched = to_row(jnp.concatenate(touched_parts, axis=0))
    steps = (rsteps[...] + 1).astype(jnp.float32)
    fix_first = 1.0 - jnp.exp(steps * jnp.log(jnp.float32(0.9)))
    fix_second = 1.0 - jnp.exp(steps * jnp.log(jnp.float32(0.95)))

    for copy in wide:
        copy.wait()
    for n, c in enumerate(issue):
        take(bufs, c, recv_sem.at[2, c])
        received = r3[c][...].reshape(ROWS, WIDTH[c])
        for rb in range(8):
            rows = pl.ds(rb * 128, 128)
            part = jnp.dot(onehot[1, rows, :], received, preferred_element_type=jnp.float32)
            folded = None
            for q in range(0, WIDTH[c], 128):
                columns = pl.ds(FIRST[c] + q, 128)
                piece = part[:, q : q + 128]
                first[rows, columns] = (
                    keep[rows, :] * moment_v[rows, columns].astype(jnp.float32) + 0.1 * piece
                )
                folded = piece * piece if folded is None else folded + piece * piece
            if n == 0:
                acc[rows, :] = folded
            else:
                acc[rows, :] += folded

    mine = to_row(jnp.sum(acc[...], axis=1, keepdims=True))
    sq_out[...] = mine
    swap = pltpu.make_async_remote_copy(
        src_ref=sq_out, dst_ref=sq_in, send_sem=sq_sem.at[0], recv_sem=sq_sem.at[1],
        device_id=partner, device_id_type=MESH,
    )
    swap.start()

    for phase in range(3):
        for c in range(CHUNKS):
            take(bufs, c, send_sem.at[phase, c])
        take(mbufs, 0, msend_sem.at[phase])
    swap.wait()

    square = (mine + sq_in[...]) / D
    live = touched > 0.0
    second = jnp.where(live, 0.95 * rscale[...] + 0.05 * square, rscale[...])
    scale[...] = second
    denom = jnp.sqrt(second / fix_second) + 1e-08
    rate = jnp.where(live, 0.01 / (fix_first * denom), 0.0)
    decay = jnp.where(live, 1.0 - 0.01 * 0.1, 1.0)
    eye = lax.broadcasted_iota(jnp.int32, (128, 128), 0) == lax.broadcasted_iota(jnp.int32, (128, 128), 1)
    for g in range(8):
        for i, value in enumerate((decay, rate)):
            column = jnp.sum(jnp.where(eye, value[g : g + 1, :], 0.0), axis=1, keepdims=True)
            coef[i, pl.ds(g * 128, 128), :] = jnp.broadcast_to(column, (128, 128))


def update(first, coef, scale, weights, new_weights, new_moment, new_scale):
    new_scale[...] = scale[...]
    for r in range(0, TALL, 16):
        rows = pl.ds(r, 16)
        decay, rate = coef[0, rows, :], coef[1, rows, :]
        for q in range(0, HALF, 128):
            columns = pl.ds(q, 128)
            value = first[rows, columns]
            new_moment[rows, columns] = value.astype(jnp.bfloat16)
            old = weights[rows, columns].astype(jnp.float32)
            new_weights[rows, columns] = (decay * old - rate * value).astype(jnp.bfloat16)


def shards(token_grads, token_slot, slot_rows, counts, weights, moment, row_scale, row_steps):
    vmem = pl.BlockSpec(memory_space=pltpu.VMEM)
    hbm = pl.BlockSpec(memory_space=pltpu.HBM)
    bf16, f32, i32 = jnp.bfloat16, jnp.float32, jnp.int32
    blocks = tuple(pltpu.VMEM((4, 4, 4, CAP, w), bf16) for w in WIDTH)
    first, coef, scale, weights_v = pl.pallas_call(
        exchange,
        name="exchange",
        out_shape=(
            pltpu.VMEM((ROWS, HALF), f32),
            pltpu.VMEM((2, ROWS, 128), f32),
            pltpu.VMEM((8, 128), f32),
            pltpu.VMEM((ROWS, HALF), bf16),
        ),
        in_specs=[hbm] * 8,
        out_specs=(vmem,) * 4,
        scratch_shapes=[
            pltpu.VMEM((8, 128), i32),
            pltpu.VMEM((1, 1024), i32),
            pltpu.VMEM((1, 64), i32),
            pltpu.VMEM((8, 128), f32),
            pltpu.VMEM((8, 128), i32),
            pltpu.VMEM((ROWS, HALF), bf16),
            pltpu.VMEM((ROWS, 128), f32),
            tuple(pltpu.VMEM((ROWS, w), bf16) for w in WIDTH),
            blocks, blocks, blocks, blocks,
            pltpu.VMEM((2, ROWS, ROWS), bf16),
            pltpu.VMEM((4, 4, 4, 1, 128), i32),
            pltpu.VMEM((4, 4, 4, 1, 128), i32),
            pltpu.VMEM((4, 4, 4, 1, 128), i32),
            pltpu.VMEM((4, 4, 4, 1, 128), i32),
            pltpu.VMEM((ROWS, 128), f32),
            pltpu.VMEM((8, 128), f32),
            pltpu.VMEM((8, 128), f32),
            pltpu.SemaphoreType.DMA((5,)),
            pltpu.SemaphoreType.DMA((2,)),
            pltpu.SemaphoreType.DMA((CHUNKS,)),
            pltpu.SemaphoreType.DMA((3, CHUNKS)),
            pltpu.SemaphoreType.DMA((3, CHUNKS)),
            pltpu.SemaphoreType.DMA((3,)),
            pltpu.SemaphoreType.DMA((3,)),
            pltpu.SemaphoreType.DMA((2,)),
        ],
        compiler_params=pltpu.CompilerParams(
            collective_id=0, has_side_effects=True, vmem_limit_bytes=38 * 1024 * 1024
        ),
        cost_estimate=pl.CostEstimate(flops=10**10, bytes_accessed=2 * 10**7, transcendentals=0),
    )(*(
        pltpu.with_memory_space_constraint(value, pltpu.HBM)
        for value in (
            token_grads, token_slot.reshape(8, 128), slot_rows, counts,
            row_scale.reshape(8, 128), row_steps.reshape(8, 128), weights, moment,
        )
    ))
    wide = pl.BlockSpec((TALL, HALF), lambda i: (i, 0))
    row = pl.BlockSpec((8, 128), lambda i: (0, 0))
    new_weights, new_moment, new_scale = pl.pallas_call(
        update,
        name="update",
        grid=(ROWS // TALL,),
        out_shape=(
            jax.ShapeDtypeStruct((ROWS, HALF), bf16),
            jax.ShapeDtypeStruct((ROWS, HALF), bf16),
            jax.ShapeDtypeStruct((8, 128), f32),
        ),
        in_specs=[wide, pl.BlockSpec((2, TALL, 128), lambda i: (0, i, 0)), row, wide],
        out_specs=(wide, wide, row),
        compiler_params=pltpu.CompilerParams(vmem_limit_bytes=10 * 1024 * 1024),
        cost_estimate=pl.CostEstimate(flops=2 * 10**7, bytes_accessed=3 * 10**7, transcendentals=0),
    )(first, coef, scale, weights_v)
    return (new_weights, new_moment, new_scale.reshape(ROWS))


def solution(mesh):
    return jax.shard_map(
        shards,
        mesh=mesh,
        in_specs=(
            P("vocab", "width"),
            P("vocab"),
            P("vocab", None),
            P("vocab", None),
            P("vocab", "width"),
            P("vocab", "width"),
            P("vocab"),
            P("vocab"),
        ),
        out_specs=(P("vocab", "width"), P("vocab", "width"), P("vocab")),
        check_vma=False,
    )
```

time: 92.4 us -> 75.5 us (0.82)
  Pallas kernels: 84.3 us -> 74.8 us
  local copies, waits for them, and re-layouts: 7.11 us -> 0 us
    pallas_call x2, Pallas kernels: 84.3 us -> 74.8 us  [the longest x1 69.3 us: shards(): pl.pallas_call(exchange, name='exchange', out_shape=(pltpu.VMEM((ROWS, HA...]
    unnamed x15 -> x0, local copies, waits for them, and re-layouts: 7.11 us -> none
where the time goes in v2:
time: 75.5 us; the launch traced here: 75.4 us
  Pallas kernels  74.8 us (99%)
    pallas_call x1, Pallas kernels, shards(): pl.pallas_call(exchange, name='exchange', out_shape=(pltpu.VMEM((ROWS, HA...  69.3 us
    pallas_call x1, Pallas kernels, shards(): pl.pallas_call(update, name='update', grid=(ROWS // TALL,), out_shape=(ja...  5.43 us

profile of v2, /device:TPU:1, one launch (start us, length us, event | category | flops | bytes accessed | tf_op | source)
XLA Modules:
  0.0 75.4 jit_solution(17439599390396593676)
XLA Ops:
  0.6 69.3 %exchange.1 = (f32[1024,2304]{1,0:T(8,128)S(1)}, f32[2,1024,128]{2,1,0:T(8,128)S(1)}, f32[8,128]{1,0:T(8,128)S(1)}, bf16[1024,2304]{1,0:T(8,128)(2,1)S(1)}) custom-call(bf16[1024,2304]{1,0:T(8,128)(2,1)} %tg.1, s32[8,128]{1,0:T(8,128)} %bitcast.4, s32[1,1024]{1,0:T(1,128)} %srows_hbm.1, s32[1,64]{1,0:T(1,128)} %cnts_hbm.1, f32[8,128]{1,0:T(8,128)} %bitcast.5, ...), custom_call_target="tpu_custom_call" | custom-call | flops 10000000000 | bytes 20000000 | tf_op jit(solution)/shard_map/exchange/pallas_call | solution.py:250
  70.0 5.4 %update.1 = (bf16[1024,2304]{1,0:T(8,128)(2,1)}, bf16[1024,2304]{1,0:T(8,128)(2,1)}, f32[8,128]{1,0:T(8,128)}) custom-call(f32[1024,2304]{1,0:T(8,128)S(1)} %get-tuple-element.10.first, f32[2,1024,128]{2,1,0:T(8,128)S(1)} %get-tuple-element.11.coef, f32[8,128]{1,0:T(8,128)S(1)} %get-tuple-element.12.scale, bf16[1024,2304]{1,0:T(8,128)(2,1)S(1)} %get-tuple-element.13.weights), custom_call_target="tpu_custom_call" | custom-call | flops 20000000 | bytes 30000000 | tf_op jit(solution)/shard_map/update/pallas_call | solution.py:301

commit v3 on v2

--- a/solution.py
+++ b/solution.py
@@ -10,8 +10,10 @@
 HALF = 2304
 ROWS = 1024
 CAP = 16
+PLANE = 128
+LINE = 208
 GROUPS = 3
-WIDTHS = (128, 256, 256, 128)
+WIDTHS = (256, 256, 256)
 PER = len(WIDTHS)
 CHUNKS = GROUPS * PER
 WIDTH = WIDTHS * GROUPS
@@ -32,10 +34,12 @@
 
 def exchange(
     tg, ts_hbm, srows_hbm, cnts_hbm, rscale_hbm, rsteps_hbm, weights, moment,
-    first, coef, scale, weights_v,
-    ts, srows, cnts, rscale, rsteps, moment_v, keep,
-    tgv, send, r1, r2, r3, onehot, ms, m1, m2, m3, acc, sq_out, sq_in,
-    small_sem, wide_sem, load_sem, send_sem, recv_sem, msend_sem, mrecv_sem, sq_sem,
+    first, coef, scale, weights_v, over,
+    ts, srows, cnts, rscale, rsteps, keep,
+    tgv, s0, r1, s1, r2, s2, r3, onehot, place, pack, unpack, pbuf,
+    ct1, ct2, flags, ms, m1, m2, m3, acc, sq_out, sq_in,
+    small_sem, wide_sem, load_sem, moment_sem, send_sem, recv_sem, msend_sem, mrecv_sem, sq_sem,
+    ct_sem, flag_sem,
 ):
     me = lax.axis_index("vocab")
     core = lax.axis_index("width")
@@ -60,10 +64,12 @@
         copy.start()
     for c in issue:
         load(c).start()
-    wide = [
-        pltpu.make_async_copy(src, dst, wide_sem.at[i])
-        for i, (src, dst) in enumerate(((weights, weights_v), (moment, moment_v)))
-    ]
+    wide = pltpu.make_async_copy(weights, weights_v, wide_sem)
+
+    def load_moment(c):
+        return pltpu.make_async_copy(
+            moment.at[:, pl.ds(FIRST[c], WIDTH[c])], tgv[c], moment_sem.at[c]
+        )
 
     barrier = pltpu.get_barrier_semaphore()
     for dim in range(3):
@@ -77,46 +83,54 @@
     for rb in range(8):
         rows = lax.broadcasted_iota(jnp.int32, (128, 128), 0) + rb * 128
         for g in range(8):
-            onehot[0, pl.ds(rb * 128, 128), pl.ds(g * 128, 128)] = (
+            onehot[pl.ds(rb * 128, 128), pl.ds(g * 128, 128)] = (
                 (rows == ts[g : g + 1, :]).astype(jnp.float32).astype(jnp.bfloat16)
             )
 
-    def leaving(buf, phase, order, c, there):
-        dim = order[phase]
+    def names_part(buf, phase, there):
         if phase == 0:
-            return (buf[c].at[there], buf[c].at[:, there], buf[c].at[:, :, there])[dim]
-        if phase == 1:
-            rest = sorted(order[1:])
-            return buf[c].at[:, there] if rest[0] == dim else buf[c].at[:, :, there]
-        return buf[c].at[:, :, there]
-
-    def landing(buf, phase, order, c):
-        dim = order[phase]
-        if phase == 0:
-            return buf[c].at[at[dim]]
-        if phase == 1:
-            seen = sorted(order[:2])
-            return buf[c].at[at[dim]] if seen[0] == dim else buf[c].at[:, at[dim]]
-        return (buf[c].at[at[dim]], buf[c].at[:, at[dim]], buf[c].at[:, :, at[dim]])[dim]
-
-    bufs = (send, r1, r2, r3)
-    mbufs = ((ms,), (m1,), (m2,), (m3,))
-
-    def forward(phase, c, order, kind, ssem, rsem):
-        src, dst = kind[phase], kind[phase + 1]
-        dim = order[phase]
+            return buf.at[there]
+        return buf.at[:, there] if phase == 1 else buf.at[:, :, there]
+
+    def post(src_of, dst, dim, ssem, rsem, own=True):
         for delta in (2, 1, 3):
             there, device = peer(dim, delta)
             pltpu.make_async_remote_copy(
-                src_ref=leaving(src, phase, order, c, there),
-                dst_ref=landing(dst, phase, order, c),
+                src_ref=src_of(there), dst_ref=dst,
                 send_sem=ssem, recv_sem=rsem, device_id=device, device_id_type=MESH,
             ).start()
-        landing(dst, phase, order, c)[...] = leaving(src, phase, order, c, at[dim])[...]
-
-    def take(kind, c, sem):
-        whole = kind[0][c].at[pl.ds(0, 3)]
+        if own:
+            dst[...] = src_of(at[dim])[...]
+
+    def post_names(phase):
+        bufs = (ms, m1, m2, m3)
+        post(
+            lambda there: names_part(bufs[phase], phase, there),
+            names_part(bufs[phase + 1], phase, at[phase]),
+            phase, msend_sem.at[phase], mrecv_sem.at[phase],
+        )
+
+    def post_rows(phase, c):
+        order = ORDERS[c // PER]
+        dim = order[phase]
+        src, dst = ((s0, r1), (s1, r2), (s2, r3))[phase]
+        if phase < 2:
+            target = dst[c].at[at[dim]]
+        else:
+            target = (dst[c].at[at[dim]], dst[c].at[:, at[dim]], dst[c].at[:, :, at[dim]])[dim]
+        post(lambda there: src[c].at[there], target, dim, send_sem.at[phase, c], recv_sem.at[phase, c])
+
+    def take(blocks, sem):
+        whole = blocks.at[pl.ds(0, 3)]
         pltpu.make_async_copy(whole, whole, sem).wait()
+
+    staged = (s0, s1, s2)
+
+    def take_rows(phase, c):
+        take(staged[phase][c], recv_sem.at[phase, c])
+
+    def coordinate(owner, dim):
+        return (owner // stride[dim]) % 4
 
     lane_g = lax.broadcasted_iota(jnp.int32, (64, 128), 1) // CAP
     own_g = lax.broadcasted_iota(jnp.int32, (64, 128), 0) % 8
@@ -136,33 +150,174 @@
             o = 8 * g + j
             ms[o // 16, (o // 4) % 4, o % 4] = turned[g : g + 1, :]
 
+
+    cnt8 = jnp.broadcast_to(cnts[...].astype(jnp.float32), (8, 64))
+    o_from = lax.broadcasted_iota(jnp.int32, (64, 64), 0)
+    o_to = lax.broadcasted_iota(jnp.int32, (64, 64), 1)
+    o_slot = lax.broadcasted_iota(jnp.int32, (8, 128), 0) * 8 + lanes // CAP
+    excess = jnp.zeros((8, 64), jnp.float32)
+    for g, (a, b, c) in enumerate(ORDERS):
+        same = coordinate(o_from, a) == coordinate(o_to, a)
+        ahead = same & (
+            coordinate(o_from, b) * 4 + coordinate(o_from, c)
+            < coordinate(o_to, b) * 4 + coordinate(o_to, c)
+        )
+        before = jnp.dot(cnt8, ahead.astype(jnp.float32), preferred_element_type=jnp.float32)
+        total = jnp.dot(cnt8, same.astype(jnp.float32), preferred_element_type=jnp.float32)
+        excess = jnp.maximum(excess, total - PLANE)
+        before = jnp.where(owner8 == lax.broadcasted_iota(jnp.int32, (8, 64), 0), before, 0.0)
+        before = jnp.dot(before, spread, preferred_element_type=jnp.float32)
+        place_at = (coordinate(o_slot, a) * PLANE + lanes % CAP).astype(jnp.float32) + before
+        high = jnp.floor(place_at * (1.0 / 32.0))
+        low = place_at - 32.0 * high
+        for blk in range(8):
+            pbuf[blk, pl.ds(2 * g, 1), :] = high[blk : blk + 1, :]
+            pbuf[blk, pl.ds(2 * g + 1, 1), :] = low[blk : blk + 1, :]
+    for blk in range(8):
+        pbuf[blk, pl.ds(6, 2), :] = jnp.zeros((2, 128), jnp.float32)
+    token_at = jnp.zeros((8, ROWS), jnp.float32)
+    for blk in range(8):
+        token_at = token_at + jnp.dot(
+            pbuf[blk].astype(jnp.bfloat16), onehot[pl.ds(blk * 128, 128), :],
+            preferred_element_type=jnp.float32,
+        )
+    for g in range(GROUPS):
+        where_to = 32.0 * token_at[2 * g : 2 * g + 1, :] + token_at[2 * g + 1 : 2 * g + 2, :]
+        for rb in range(0, 4 * PLANE, 128):
+            rows = (lax.broadcasted_iota(jnp.int32, (128, ROWS), 0) + rb).astype(jnp.float32)
+            place[g, pl.ds(rb, 128), :] = (rows == where_to).astype(jnp.float32).astype(jnp.bfloat16)
+
     pl.semaphore_wait(barrier, 10)
-    forward(0, 0, ORDERS[0], mbufs, msend_sem.at[0], mrecv_sem.at[0])
+    for dim in range(3):
+        post(lambda there: cnts, ct1.at[dim, at[dim]], dim, ct_sem.at[0, dim], ct_sem.at[1, dim])
+    post_names(0)
 
     for c in issue:
         load(c).wait()
-        send[c][...] = (
-            jnp.dot(onehot[0], tgv[c][...], preferred_element_type=jnp.float32)
+        s0[c][...] = (
+            jnp.dot(place[c // PER], tgv[c][...], preferred_element_type=jnp.float32)
+            .astype(jnp.bfloat16)
+            .reshape(4, PLANE, WIDTH[c])
+        )
+        post_rows(0, c)
+
+    b_of = lax.broadcasted_iota(jnp.int32, (8, 64), 0)
+    o_line = lax.broadcasted_iota(jnp.int32, (8, 64), 1)
+    ones = jnp.ones((64, 128), jnp.float32)
+    excess = jnp.max(jnp.max(excess, axis=1, keepdims=True), axis=0, keepdims=True)
+    idx = lanes.astype(jnp.float32)
+    line_at = (lax.broadcasted_iota(jnp.int32, (8, 128), 0) * LINE).astype(jnp.float32)
+    for dim in range(3):
+        take(ct1.at[dim], ct_sem.at[1, dim])
+    for g, (a, b, c) in enumerate(ORDERS):
+        post(
+            lambda there: ct1.at[a], ct2.at[g, at[b]], b, ct_sem.at[2, g], ct_sem.at[3, g]
+        )
+        in_plane = coordinate(o_line, a) == at[a]
+        b_owner = coordinate(o_line, b)
+        base = jnp.zeros((8, 128), jnp.float32)
+        for source in range(4):
+            row = jnp.broadcast_to(ct1[a, source].astype(jnp.float32), (8, 64))
+            offset = jnp.dot(
+                jnp.where(in_plane & (b_owner < b_of), row, 0.0), ones, preferred_element_type=jnp.float32
+            )
+            length = jnp.dot(
+                jnp.where(in_plane & (b_owner == b_of), row, 0.0), ones, preferred_element_type=jnp.float32
+            )
+            inside = (idx >= offset) & (idx < offset + length)
+            goes = jnp.sum(
+                jnp.where(inside, line_at + base + idx - offset + 1.0, 0.0), axis=0, keepdims=True
+            )
+            for rb in range(0, 4 * LINE, 208):
+                rows = (lax.broadcasted_iota(jnp.int32, (208, 128), 0) + (rb + 1)).astype(jnp.float32)
+                pack[g, pl.ds(rb, 208), pl.ds(source * 128, 128)] = (
+                    (rows == goes).astype(jnp.float32).astype(jnp.bfloat16)
+                )
+            base = base + length
+        most = jnp.max(base - LINE, axis=0, keepdims=True)
+        excess = jnp.maximum(excess, most)
+    flags[0, at[0]] = jnp.where(excess > 0.0, 1, 0)
+
+    def post_flag(dim):
+        post(
+            lambda there: flags.at[dim, at[dim]], flags.at[dim, at[dim]], dim,
+            flag_sem.at[0, dim], flag_sem.at[1, dim], own=False,
+        )
+
+    take(m1, mrecv_sem.at[0])
+    post_names(1)
+    for n, c in enumerate(issue):
+        take_rows(0, c)
+        s1[c][...] = (
+            jnp.dot(pack[c // PER], r1[c][...].reshape(4 * PLANE, WIDTH[c]), preferred_element_type=jnp.float32)
+            .astype(jnp.bfloat16)
+            .reshape(4, LINE, WIDTH[c])
+        )
+        post_rows(1, c)
+        load_moment(c).start()
+        if n == 0:
+            post_flag(0)
+        if n == 2:
+            take(m1, mrecv_sem.at[1])
+            post_names(2)
+            take(flags.at[0], flag_sem.at[1, 0])
+            flags[1, at[1]] = jnp.max(flags[0], axis=0)
+        if n == 3:
+            post_flag(1)
+        if n == 5:
+            take(flags.at[1], flag_sem.at[1, 1])
+            flags[2, at[2]] = jnp.max(flags[1], axis=0)
+        if n == 6:
+            post_flag(2)
+    wide.start()
+
+    unit = lax.broadcasted_iota(jnp.int32, (64, 64), 0)
+    slot_unit = (
+        lax.broadcasted_iota(jnp.int32, (ROWS, 64), 0) // CAP == lax.broadcasted_iota(jnp.int32, (ROWS, 64), 1)
+    ).astype(jnp.float32)
+    slot = lax.broadcasted_iota(jnp.int32, (ROWS, 128), 0)
+    for g, (a, b, c) in enumerate(ORDERS):
+        take(ct2.at[g], ct_sem.at[3, g])
+        c_unit = unit // 16
+        a_unit, b_unit = ((unit // 4) % 4, unit % 4) if a < b else (unit % 4, (unit // 4) % 4)
+        in_line = (coordinate(o_to, a) == at[a]) & (coordinate(o_to, b) == at[b])
+        c_owner = coordinate(o_to, c)
+        begin = jnp.zeros((64, 64), jnp.float32)
+        size = jnp.zeros((64, 64), jnp.float32)
+        for sb in range(4):
+            for sa in range(4):
+                row = jnp.broadcast_to(ct2[g, sb, sa].astype(jnp.float32), (64, 64))
+                row = jnp.where(in_line & (b_unit == sb), row, 0.0)
+                begin = begin + jnp.where(
+                    (a_unit > sa) | ((a_unit == sa) & (c_owner < c_unit)), row, 0.0
+                )
+                size = size + jnp.where((a_unit == sa) & (c_owner == c_unit), row, 0.0)
+        begin = jnp.dot(begin, ones, preferred_element_type=jnp.float32)
+        size = jnp.dot(size, ones, preferred_element_type=jnp.float32)
+        begin = jnp.dot(slot_unit, begin, preferred_element_type=jnp.float32)
+        size = jnp.dot(slot_unit, size, preferred_element_type=jnp.float32)
+        within = (slot % CAP).astype(jnp.float32)
+        sb_slot = (slot // CAP) % 4 if a < b else (slot // (CAP * 4)) % 4
+        comes = jnp.where(
+            within < size, (sb_slot * LINE).astype(jnp.float32) + begin + within, -1.0
+        )
+        for q in range(0, 4 * LINE, 128):
+            span = min(128, 4 * LINE - q)
+            columns = (lax.broadcasted_iota(jnp.int32, (ROWS, span), 1) + q).astype(jnp.float32)
+            unpack[g, :, pl.ds(q, span)] = (
+                (columns == comes[:, :span]).astype(jnp.float32).astype(jnp.bfloat16)
+            )
+
+    for c in issue:
+        take_rows(1, c)
+        s2[c][...] = (
+            jnp.dot(unpack[c // PER], r2[c][...].reshape(4 * LINE, WIDTH[c]), preferred_element_type=jnp.float32)
             .astype(jnp.bfloat16)
             .reshape(4, 4, 4, CAP, WIDTH[c])
         )
-        forward(0, c, ORDERS[c // PER], bufs, send_sem.at[0, c], recv_sem.at[0, c])
-
-    for copy in wide:
-        copy.start()
-    take(mbufs, 0, mrecv_sem.at[0])
-    forward(1, 0, ORDERS[0], mbufs, msend_sem.at[1], mrecv_sem.at[1])
-    for n, c in enumerate(issue):
-        take(bufs, c, recv_sem.at[0, c])
-        forward(1, c, ORDERS[c // PER], bufs, send_sem.at[1, c], recv_sem.at[1, c])
-        if n == 2:
-            take(mbufs, 0, mrecv_sem.at[1])
-            forward(2, 0, ORDERS[0], mbufs, msend_sem.at[2], mrecv_sem.at[2])
-    for c in issue:
-        take(bufs, c, recv_sem.at[1, c])
-        forward(2, c, ORDERS[c // PER], bufs, send_sem.at[2, c], recv_sem.at[2, c])
-
-    take(mbufs, 0, mrecv_sem.at[2])
+        post_rows(2, c)
+
+    take(m1, mrecv_sem.at[2])
     named = m3[...].reshape(8, 8, 128).sum(axis=1)
     touched_parts = []
     for rb in range(8):
@@ -170,7 +325,7 @@
         any_hit = jnp.zeros((128, 128), jnp.float32)
         for g in range(8):
             hit = (rows == named[g : g + 1, :]).astype(jnp.float32)
-            onehot[1, pl.ds(rb * 128, 128), pl.ds(g * 128, 128)] = hit.astype(jnp.bfloat16)
+            onehot[pl.ds(rb * 128, 128), pl.ds(g * 128, 128)] = hit.astype(jnp.bfloat16)
             any_hit = jnp.maximum(any_hit, hit)
         hit_column = jnp.max(any_hit, axis=1, keepdims=True)
         touched_parts.append(hit_column)
@@ -180,20 +335,19 @@
     fix_first = 1.0 - jnp.exp(steps * jnp.log(jnp.float32(0.9)))
     fix_second = 1.0 - jnp.exp(steps * jnp.log(jnp.float32(0.95)))
 
-    for copy in wide:
-        copy.wait()
     for n, c in enumerate(issue):
-        take(bufs, c, recv_sem.at[2, c])
+        take_rows(2, c)
+        load_moment(c).wait()
         received = r3[c][...].reshape(ROWS, WIDTH[c])
         for rb in range(8):
             rows = pl.ds(rb * 128, 128)
-            part = jnp.dot(onehot[1, rows, :], received, preferred_element_type=jnp.float32)
+            part = jnp.dot(onehot[rows, :], received, preferred_element_type=jnp.float32)
             folded = None
             for q in range(0, WIDTH[c], 128):
                 columns = pl.ds(FIRST[c] + q, 128)
                 piece = part[:, q : q + 128]
                 first[rows, columns] = (
-                    keep[rows, :] * moment_v[rows, columns].astype(jnp.float32) + 0.1 * piece
+                    keep[rows, :] * tgv[c][rows, pl.ds(q, 128)].astype(jnp.float32) + 0.1 * piece
                 )
                 folded = piece * piece if folded is None else folded + piece * piece
             if n == 0:
@@ -211,8 +365,14 @@
 
     for phase in range(3):
         for c in range(CHUNKS):
-            take(bufs, c, send_sem.at[phase, c])
-        take(mbufs, 0, msend_sem.at[phase])
+            take(staged[phase][c], send_sem.at[phase, c])
+        take(m1, msend_sem.at[phase])
+        take(ct1.at[0], ct_sem.at[0, phase])
+        take(ct2.at[0], ct_sem.at[2, phase])
+        take(flags.at[0], flag_sem.at[0, phase])
+    take(flags.at[2], flag_sem.at[1, 2])
+    over[...] = jnp.max(flags[2], axis=0)
+    wide.wait()
     swap.wait()
 
     square = (mine + sq_in[...]) / D
@@ -242,12 +402,56 @@
             new_weights[rows, columns] = (decay * old - rate * value).astype(jnp.bfloat16)
 
 
+def over_pieces(value, axis):
+    parts = lax.all_gather(value, axis)
+    return parts.sum(axis=0)
+
+
+def any_counts(token_grads, token_slot, slot_rows, counts, weights, moment, row_scale, row_steps):
+    owners = lax.axis_size("vocab")
+    slots_all = slot_rows.shape[1]
+    cap = slots_all // owners
+    half = token_grads.shape[1]
+    rows_own = weights.shape[0]
+    placing = token_slot[None, :] == jnp.arange(slots_all, dtype=jnp.int32)[:, None]
+    slot_grads = jnp.dot(
+        placing.astype(jnp.bfloat16), token_grads, preferred_element_type=jnp.float32
+    ).astype(jnp.bfloat16)
+    within = jnp.arange(cap, dtype=jnp.int32)
+    live = within[None, :] < counts[0][:, None]
+    named = jnp.where(live, slot_rows[0].reshape(owners, cap), -1)
+    outgoing = slot_grads.reshape(owners, cap, half)
+    received, received_rows = (
+        lax.all_to_all(outgoing, "vocab", split_axis=0, concat_axis=0, tiled=True),
+        lax.all_to_all(named, "vocab", split_axis=0, concat_axis=0, tiled=True),
+    )
+    flat = received.reshape(owners * cap, half)
+    flat_rows = received_rows.reshape(owners * cap)
+    table = flat_rows[None, :] == jnp.arange(rows_own, dtype=jnp.int32)[:, None]
+    grad = jnp.dot(table.astype(jnp.bfloat16), flat, preferred_element_type=jnp.float32)
+    hits = jnp.sum(table.astype(jnp.int32), axis=1)
+    touched = hits > 0
+    partial_sum = jnp.sum(grad * grad, axis=1)
+    square = over_pieces(partial_sum, "width") / D
+    step_count = (row_steps + 1).astype(jnp.float32)
+    old_moment = moment.astype(jnp.float32)
+    first = jnp.where(touched[:, None], 0.9 * old_moment + 0.1 * grad, old_moment)
+    second = jnp.where(touched, 0.95 * row_scale + 0.05 * square, row_scale)
+    fix_first = 1.0 - jnp.power(jnp.float32(0.9), step_count)
+    fix_second = 1.0 - jnp.power(jnp.float32(0.95), step_count)
+    denom = jnp.sqrt(second / fix_second) + 1e-08
+    old = weights.astype(jnp.float32)
+    stepped = old - 0.01 * (first / fix_first[:, None] / denom[:, None] + 0.1 * old)
+    new_weights = jnp.where(touched[:, None], stepped, old).astype(jnp.bfloat16)
+    return (new_weights, first.astype(jnp.bfloat16), second)
+
+
 def shards(token_grads, token_slot, slot_rows, counts, weights, moment, row_scale, row_steps):
     vmem = pl.BlockSpec(memory_space=pltpu.VMEM)
     hbm = pl.BlockSpec(memory_space=pltpu.HBM)
     bf16, f32, i32 = jnp.bfloat16, jnp.float32, jnp.int32
     blocks = tuple(pltpu.VMEM((4, 4, 4, CAP, w), bf16) for w in WIDTH)
-    first, coef, scale, weights_v = pl.pallas_call(
+    first, coef, scale, weights_v, over = pl.pallas_call(
         exchange,
         name="exchange",
         out_shape=(
@@ -255,20 +459,32 @@
             pltpu.VMEM((2, ROWS, 128), f32),
             pltpu.VMEM((8, 128), f32),
             pltpu.VMEM((ROWS, HALF), bf16),
+            jax.ShapeDtypeStruct((1, 128), i32),
         ),
         in_specs=[hbm] * 8,
-        out_specs=(vmem,) * 4,
+        out_specs=(vmem,) * 5,
         scratch_shapes=[
             pltpu.VMEM((8, 128), i32),
             pltpu.VMEM((1, 1024), i32),
             pltpu.VMEM((1, 64), i32),
             pltpu.VMEM((8, 128), f32),
             pltpu.VMEM((8, 128), i32),
-            pltpu.VMEM((ROWS, HALF), bf16),
             pltpu.VMEM((ROWS, 128), f32),
             tuple(pltpu.VMEM((ROWS, w), bf16) for w in WIDTH),
-            blocks, blocks, blocks, blocks,
-            pltpu.VMEM((2, ROWS, ROWS), bf16),
+            tuple(pltpu.VMEM((4, PLANE, w), bf16) for w in WIDTH),
+            tuple(pltpu.VMEM((4, PLANE, w), bf16) for w in WIDTH),
+            tuple(pltpu.VMEM((4, LINE, w), bf16) for w in WIDTH),
+            tuple(pltpu.VMEM((4, LINE, w), bf16) for w in WIDTH),
+            blocks,
+            blocks,
+            pltpu.VMEM((ROWS, ROWS), bf16),
+            pltpu.VMEM((GROUPS, 4 * PLANE, ROWS), bf16),
+            pltpu.VMEM((GROUPS, 4 * LINE, 4 * PLANE), bf16),
+            pltpu.VMEM((GROUPS, ROWS, 4 * LINE), bf16),
+            pltpu.VMEM((8, 8, 128), f32),
+            pltpu.VMEM((3, 4, 1, 64), i32),
+            pltpu.VMEM((3, 4, 4, 1, 64), i32),
+            pltpu.VMEM((3, 4, 1, 128), i32),
             pltpu.VMEM((4, 4, 4, 1, 128), i32),
             pltpu.VMEM((4, 4, 4, 1, 128), i32),
             pltpu.VMEM((4, 4, 4, 1, 128), i32),
@@ -277,16 +493,19 @@
             pltpu.VMEM((8, 128), f32),
             pltpu.VMEM((8, 128), f32),
             pltpu.SemaphoreType.DMA((5,)),
-            pltpu.SemaphoreType.DMA((2,)),
+            pltpu.SemaphoreType.DMA,
+            pltpu.SemaphoreType.DMA((CHUNKS,)),
             pltpu.SemaphoreType.DMA((CHUNKS,)),
             pltpu.SemaphoreType.DMA((3, CHUNKS)),
             pltpu.SemaphoreType.DMA((3, CHUNKS)),
             pltpu.SemaphoreType.DMA((3,)),
             pltpu.SemaphoreType.DMA((3,)),
             pltpu.SemaphoreType.DMA((2,)),
+            pltpu.SemaphoreType.DMA((4, 3)),
+            pltpu.SemaphoreType.DMA((2, 3)),
         ],
         compiler_params=pltpu.CompilerParams(
-            collective_id=0, has_side_effects=True, vmem_limit_bytes=38 * 1024 * 1024
+            collective_id=0, has_side_effects=True, vmem_limit_bytes=46 * 1024 * 1024
         ),
         cost_estimate=pl.CostEstimate(flops=10**10, bytes_accessed=2 * 10**7, transcendentals=0),
     )(*(
@@ -312,7 +531,12 @@
         compiler_params=pltpu.CompilerParams(vmem_limit_bytes=10 * 1024 * 1024),
         cost_estimate=pl.CostEstimate(flops=2 * 10**7, bytes_accessed=3 * 10**7, transcendentals=0),
     )(first, coef, scale, weights_v)
-    return (new_weights, new_moment, new_scale.reshape(ROWS))
+    arguments = (token_grads, token_slot, slot_rows, counts, weights, moment, row_scale, row_steps)
+    return lax.while_loop(
+        lambda state: state[3] > 0,
+        lambda state: any_counts(*arguments) + (jnp.int32(0),),
+        (new_weights, new_moment, new_scale.reshape(ROWS), over[0, 0]),
+    )[:3]
 
 
 def solution(mesh):

time: 75.5 us -> 66.9 us (0.89)
  Pallas kernels: 74.8 us -> 65.1 us
  loops' own time: 0 us -> 0.85 us
    pallas_call x1, Pallas kernels: 69.3 us -> 59.7 us  [shards(): pl.pallas_call(exchange, name='exchange', out_shape=(pltpu.VMEM((ROWS, HA...]
    another operation x0 -> x1, loops' own time: none -> 0.85 us  [shards(): lax.while_loop(lambda state: state[3] > 0, lambda state: any_counts(*argu...]
where the time goes in v3:
time: 66.9 us; the launch traced here: 66.8 us
  Pallas kernels  65.1 us (97%)
  between operations  0.89 us (1%)
  loops' own time  0.85 us (1%)
    pallas_call x1, Pallas kernels, shards(): pl.pallas_call(exchange, name='exchange', out_shape=(pltpu.VMEM((ROWS, HA...  59.7 us
    pallas_call x1, Pallas kernels, shards(): pl.pallas_call(update, name='update', grid=(ROWS // TALL,), out_shape=(ja...  5.39 us

profile of v3, /device:TPU:1, one launch (start us, length us, event | category | flops | bytes accessed | tf_op | source)
XLA Modules:
  0.0 66.8 jit_solution(8700738692787659057)
XLA Ops:
  0.6 59.7 %exchange.1 = (f32[1024,2304]{1,0:T(8,128)S(1)}, f32[2,1024,128]{2,1,0:T(8,128)S(1)}, f32[8,128]{1,0:T(8,128)S(1)}, bf16[1024,2304]{1,0:T(8,128)(2,1)S(1)}, s32[1,128]{1,0:T(1,128)}) custom-call(bf16[1024,2304]{1,0:T(8,128)(2,1)} %tg.1, s32[8,128]{1,0:T(8,128)} %bitcast.16, s32[1,1024]{1,0:T(1,128)} %srows_hbm.1, s32[1,64]{1,0:T(1,128)} %cnts_hbm.1, ...), custom_call_target="tpu_custom_call" | custom-call | flops 10000000000 | bytes 20000000 | tf_op jit(solution)/shard_map/exchange/pallas_call | solution.py:454
  60.3 0.0 copy-start
  60.3 0.0 copy-start.1
  60.3 0.0 copy-start.2
  60.3 0.0 copy-start.3
  60.4 0.0 copy-start.4
  60.4 5.4 %update.1 = (bf16[1024,2304]{1,0:T(8,128)(2,1)}, bf16[1024,2304]{1,0:T(8,128)(2,1)}, f32[8,128]{1,0:T(8,128)}) custom-call(f32[1024,2304]{1,0:T(8,128)S(1)} %get-tuple-element.71.first, f32[2,1024,128]{2,1,0:T(8,128)S(1)} %get-tuple-element.72.coef, f32[8,128]{1,0:T(8,128)S(1)} %get-tuple-element.73.scale, bf16[1024,2304]{1,0:T(8,128)(2,1)S(1)} %get-tuple-element.74.weights), custom_call_target="tpu_custom_call" | custom-call | flops 20000000 | bytes 30000000 | tf_op jit(solution)/shard_map/update/pallas_call | solution.py:520
  65.8 0.0 copy-done
  65.8 0.0 copy-done.1
  65.8 0.0 copy-done.2
  65.8 0.0 copy-done.3
  65.8 0.0 copy-done.4
  65.8 0.8 %while.13 = (bf16[1024,2304]{1,0:T(8,128)(2,1)}, bf16[1024,2304]{1,0:T(8,128)(2,1)}, f32[1024]{0:T(1024)}, s32[]{:T(128)}, s32[1,64]{1,0:T(1,128)S(1)}, /*index=...) while((bf16[1024,2304]{1,0:T(8,128)(2,1)}, ...), condition=%region_4.5_spmd, body=%region_0.4_spmd | while | flops 9709040640 | bytes 66263492 | solution.py:535
Async XLA Ops:
  60.3 5.4 %copy-start = (f32[1024]{0:T(1024)S(1)}, f32[1024]{0:T(1024)}, u32[]{:S(2)}) copy-start(f32[1024]{0:T(1024)} %param.16) | copy-start | bytes 12292
  60.3 5.4 %copy-start.1 = (s32[1024]{0:T(1024)S(1)}, s32[1024]{0:T(1024)}, u32[]{:S(2)}) copy-start(s32[1024]{0:T(1024)} %param.17) | copy-start | bytes 12292
  60.3 5.4 %copy-start.2 = (s32[1,1024]{1,0:T(1,128)S(1)}, s32[1,1024]{1,0:T(1,128)}, u32[]{:S(2)}) copy-start(s32[1,1024]{1,0:T(1,128)} %srows_hbm.1) | copy-start | bytes 12292
  60.3 5.4 %copy-start.3 = (s32[1,64]{1,0:T(1,128)S(1)}, s32[1,64]{1,0:T(1,128)}, u32[]{:S(2)}) copy-start(s32[1,64]{1,0:T(1,128)} %cnts_hbm.1) | copy-start | bytes 772
  60.4 5.4 %copy-start.4 = (s32[1024]{0:T(1024)S(1)}, s32[1024]{0:T(1024)}, u32[]{:S(2)}) copy-start(s32[1024]{0:T(1024)} %param.11) | copy-start | bytes 12292

commit v4 on v3

--- a/solution.py
+++ b/solution.py
@@ -18,7 +18,7 @@
 CHUNKS = GROUPS * PER
 WIDTH = WIDTHS * GROUPS
 FIRST = tuple(sum(WIDTH[:c]) for c in range(CHUNKS))
-TALL = 128
+TALL = 64
 MESH = pl.DeviceIdType.MESH
 ORDERS = ((0, 1, 2), (1, 2, 0), (2, 0, 1))
 
@@ -389,17 +389,32 @@
             coef[i, pl.ds(g * 128, 128), :] = jnp.broadcast_to(column, (128, 128))
 
 
-def update(first, coef, scale, weights, new_weights, new_moment, new_scale):
-    new_scale[...] = scale[...]
-    for r in range(0, TALL, 16):
-        rows = pl.ds(r, 16)
-        decay, rate = coef[0, rows, :], coef[1, rows, :]
-        for q in range(0, HALF, 128):
-            columns = pl.ds(q, 128)
-            value = first[rows, columns]
-            new_moment[rows, columns] = value.astype(jnp.bfloat16)
-            old = weights[rows, columns].astype(jnp.float32)
-            new_weights[rows, columns] = (decay * old - rate * value).astype(jnp.bfloat16)
+def update(first, coef, scale, weights, new_weights, new_moment, new_scale, made_w, made_m, sem, scale_sem):
+    out_scale = pltpu.make_async_copy(scale, new_scale, scale_sem)
+    out_scale.start()
+    copies = []
+    for n in range(ROWS // TALL):
+        block = pl.ds(n * TALL, TALL)
+
+        def some(r, carry, n=n):
+            rows = pl.ds(pl.multiple_of(n * TALL + r * 16, 16), 16)
+            decay, rate = coef[0, rows, :], coef[1, rows, :]
+            for q in range(0, HALF, 128):
+                columns = pl.ds(q, 128)
+                value = first[rows, columns]
+                made_m[rows, columns] = value.astype(jnp.bfloat16)
+                old = weights[rows, columns].astype(jnp.float32)
+                made_w[rows, columns] = (decay * old - rate * value).astype(jnp.bfloat16)
+            return carry
+
+        lax.fori_loop(0, TALL // 16, some, 0)
+        for i, (src, dst) in enumerate(((made_m, new_moment), (made_w, new_weights))):
+            copy = pltpu.make_async_copy(src.at[block, :], dst.at[block, :], sem.at[i, n])
+            copy.start()
+            copies.append(copy)
+    for copy in copies:
+        copy.wait()
+    out_scale.wait()
 
 
 def over_pieces(value, axis):
@@ -515,20 +530,23 @@
             row_scale.reshape(8, 128), row_steps.reshape(8, 128), weights, moment,
         )
     ))
-    wide = pl.BlockSpec((TALL, HALF), lambda i: (i, 0))
-    row = pl.BlockSpec((8, 128), lambda i: (0, 0))
     new_weights, new_moment, new_scale = pl.pallas_call(
         update,
         name="update",
-        grid=(ROWS // TALL,),
         out_shape=(
             jax.ShapeDtypeStruct((ROWS, HALF), bf16),
             jax.ShapeDtypeStruct((ROWS, HALF), bf16),
             jax.ShapeDtypeStruct((8, 128), f32),
         ),
-        in_specs=[wide, pl.BlockSpec((2, TALL, 128), lambda i: (0, i, 0)), row, wide],
-        out_specs=(wide, wide, row),
-        compiler_params=pltpu.CompilerParams(vmem_limit_bytes=10 * 1024 * 1024),
+        in_specs=[vmem] * 4,
+        out_specs=(hbm,) * 3,
+        scratch_shapes=[
+            pltpu.VMEM((ROWS, HALF), bf16),
+            pltpu.VMEM((ROWS, HALF), bf16),
+            pltpu.SemaphoreType.DMA((2, ROWS // TALL)),
+            pltpu.SemaphoreType.DMA,
+        ],
+        compiler_params=pltpu.CompilerParams(vmem_limit_bytes=12 * 1024 * 1024),
         cost_estimate=pl.CostEstimate(flops=2 * 10**7, bytes_accessed=3 * 10**7, transcendentals=0),
     )(first, coef, scale, weights_v)
     arguments = (token_grads, token_slot, slot_rows, counts, weights, moment, row_scale, row_steps)

time: 66.9 us -> 65.6 us (0.981)
  Pallas kernels: 65.1 us -> 63.9 us
    pallas_call x1, Pallas kernels: 5.39 us -> 4.24 us  [shards(): pl.pallas_call(update, name='update', out_shape=(jax.ShapeDtypeStruct((RO...]
where the time goes in v4:
time: 65.6 us; the launch traced here: 65.5 us
  Pallas kernels  63.9 us (97%)
  between operations  0.9 us (1%)
    pallas_call x1, Pallas kernels, shards(): pl.pallas_call(exchange, name='exchange', out_shape=(pltpu.VMEM((ROWS, HA...  59.7 us
    pallas_call x1, Pallas kernels, shards(): pl.pallas_call(update, name='update', out_shape=(jax.ShapeDtypeStruct((RO...  4.24 us

profile of v4, /device:TPU:1, one launch (start us, length us, event | category | flops | bytes accessed | tf_op | source)
XLA Modules:
  0.0 65.5 jit_solution(4748305653017185549)
XLA Ops:
  0.6 59.7 %exchange.1 = (f32[1024,2304]{1,0:T(8,128)S(1)}, f32[2,1024,128]{2,1,0:T(8,128)S(1)}, f32[8,128]{1,0:T(8,128)S(1)}, bf16[1024,2304]{1,0:T(8,128)(2,1)S(1)}, s32[1,128]{1,0:T(1,128)}) custom-call(bf16[1024,2304]{1,0:T(8,128)(2,1)} %tg.1, s32[8,128]{1,0:T(8,128)} %bitcast.16, s32[1,1024]{1,0:T(1,128)} %srows_hbm.1, s32[1,64]{1,0:T(1,128)} %cnts_hbm.1, ...), custom_call_target="tpu_custom_call" | custom-call | flops 10000000000 | bytes 20000000 | tf_op jit(solution)/shard_map/exchange/pallas_call | solution.py:469
  60.3 0.0 copy-start
  60.3 0.0 copy-start.1
  60.3 0.0 copy-start.2
  60.3 0.0 copy-start.3
  60.4 0.0 copy-start.4
  60.4 4.2 %update.1 = (bf16[1024,2304]{1,0:T(8,128)(2,1)}, bf16[1024,2304]{1,0:T(8,128)(2,1)}, f32[8,128]{1,0:T(8,128)}) custom-call(f32[1024,2304]{1,0:T(8,128)S(1)} %get-tuple-element.71.first, f32[2,1024,128]{2,1,0:T(8,128)S(1)} %get-tuple-element.72.coef, f32[8,128]{1,0:T(8,128)S(1)} %get-tuple-element.73.scale, bf16[1024,2304]{1,0:T(8,128)(2,1)S(1)} %get-tuple-element.74.weights), custom_call_target="tpu_custom_call" | custom-call | flops 20000000 | bytes 30000000 | tf_op jit(solution)/shard_map/update/pallas_call | solution.py:533
  64.6 0.0 copy-done
  64.6 0.0 copy-done.1
  64.6 0.0 copy-done.2
  64.6 0.0 copy-done.3
  64.7 0.0 copy-done.4
  64.7 0.6 while.13
Async XLA Ops:
  60.3 4.3 %copy-start = (f32[1024]{0:T(1024)S(1)}, f32[1024]{0:T(1024)}, u32[]{:S(2)}) copy-start(f32[1024]{0:T(1024)} %param.16) | copy-start | bytes 12292
  60.3 4.3 %copy-start.1 = (s32[1024]{0:T(1024)S(1)}, s32[1024]{0:T(1024)}, u32[]{:S(2)}) copy-start(s32[1024]{0:T(1024)} %param.17) | copy-start | bytes 12292
  60.3 4.3 %copy-start.2 = (s32[1,1024]{1,0:T(1,128)S(1)}, s32[1,1024]{1,0:T(1,128)}, u32[]{:S(2)}) copy-start(s32[1,1024]{1,0:T(1,128)} %srows_hbm.1) | copy-start | bytes 12292
  60.3 4.3 %copy-start.3 = (s32[1,64]{1,0:T(1,128)S(1)}, s32[1,64]{1,0:T(1,128)}, u32[]{:S(2)}) copy-start(s32[1,64]{1,0:T(1,128)} %cnts_hbm.1) | copy-start | bytes 772
  60.4 4.3 %copy-start.4 = (s32[1024]{0:T(1024)S(1)}, s32[1024]{0:T(1024)}, u32[]{:S(2)}) copy-start(s32[1024]{0:T(1024)} %param.11) | copy-start | bytes 12292
